TPU v7x, 128 devices: a whole 4x4x4 slice. The times are simulated.
128 devices in a mesh: grp: 4 (over z_hi, core), row: 4 (over y), col: 8 (over x, z_lo).
Axes of the slice: x: 4, y: 4, z: 4 (z_hi: 2, z_lo: 2; z = z_hi * 2 + z_lo), core: 2. Of those that a mesh axis runs over, the one named last changes fastest.
Arguments:
- tokens: bfloat16 [8192, 4608], P(('grp', 'row', 'col')), parts along dimension 0, may hold values from -6 to 6
- ln_gain: float32 [4608], replicated, may hold values from 0.1 to 1.9
- w_in: bfloat16 [4608, 12288], P('row', 'col'), may hold values from -0.09375 to 0.09375
- b_in: float32 [12288], P('col'), may hold values from -3 to 3
- w_out: bfloat16 [12288, 4608], P('col', 'row'), may hold values from -0.0546875 to 0.0546875
- b_out: float32 [4608], P('row'), may hold values from -3 to 3
Outputs:
- result: bfloat16 [8192, 4608], P(('grp', 'row', 'col')), parts along dimension 0
There are 4 independent parts, one for each index of `grp`. A program takes and returns all parts, laid end to end along the dimension named above; an argument that names none is the same for every part. Nothing has to cross between parts.
All inputs are finite; a program needn't handle non-finite values.
Results may differ from a plain program's by a relative error of at most 0.0095.
Values may be sent and summed in bfloat16 or wider, within the bound.
A program may use at most 128 MiB of HBM per device.

v0:
```python
import functools

import jax
import jax.numpy as jnp
from jax import lax
from jax.experimental import pallas as pl
from jax.experimental.pallas import tpu as pltpu
from jax.sharding import PartitionSpec as P

MESH = pl.DeviceIdType.MESH
F32, BF16 = jnp.float32, jnp.bfloat16
NQ = 4
N_RECV = 155
SQRT_HALF = 0.7071067811865476
OWN, UP, DOWN, FAR = 0, 1, 2, 3
C1 = 128
W1_CHUNKS = ((0, 1, 2), (1, 1, 4), (2, 2, 2), (4, 2, 4), (6, 2, 2), (8, 2, 4), (10, 2, 4))
NW2 = 9
Z = (0, 2)
OWN01, NEAR0, FAR0 = ((0, 1), (0, 2), Z), ((1, 3), (0, 1), Z), ((3, 4), (0, 1), Z)
REST0, REST1, REST2 = ((1, 4), (0, 1), Z), ((1, 4), (1, 2), Z), ((1, 4), (2, 3), Z)
NEAR3, FAR3 = ((1, 3), (3, 4), Z), ((3, 4), (3, 4), Z)
OWN23, OWN23Z1, OWN23Z0 = ((0, 1), (2, 4), Z), ((0, 1), (2, 4), (1, 2)), ((0, 1), (2, 4), (0, 1))


def kernel(dims, tok_hbm, gain_hbm, w1_hbm, b1_hbm, w2_hbm, b2_hbm, out,
           tok, gain, b1, b2_own, w1, w2, x, nb, p32, ps, pr, hid, os_, r1, r2, zs, zr, fs, fr, b2_far,
           send_sems, recv_sems, local_sems):
    tq, kb, nf = dims
    nx = 4
    width = nx * kb

    grp, y, col = lax.axis_index("grp"), lax.axis_index("row"), lax.axis_index("col")
    xx, z, core, half = col // 2, col % 2, grp % 2, grp // 2
    m = y % 2
    y_pair = y + 1 - 2 * m
    y_far = 3 - y
    x_up, x_dn = (xx + 1) % 4, (xx + 3) % 4
    core_grp = grp + 1 - 2 * core
    twin_grp = grp + 2 - 4 * half
    diag_grp = core_grp + 2 - 4 * half
    DEV = {
        "pair": (grp, y_pair, col),
        "far": (grp, y_far, col),
        "core": (core_grp, y, col),
        "twin": (twin_grp, y, col),
        "up": (grp, y, x_up * 2 + z),
        "dn": (grp, y, x_dn * 2 + z),
        "z": (grp, y, xx * 2 + 1 - z),
    }
    my_blocks = (y, y_far)
    pair_blocks = (y_pair, 3 - y_pair)

    def lanes(block):
        return pl.ds(pl.multiple_of(block * kb, 128), kb)

    ids, landing, waited, groups = {}, {}, set(), {}

    def send(key, src, dst, to, landed=None, group=None):
        i = ids.setdefault(key, len(ids))
        g = groups.setdefault(group or key[0], len(groups))
        landing[key] = (dst if landed is None else landed, to, i)
        pltpu.make_async_remote_copy(
            src_ref=src, dst_ref=dst, send_sem=send_sems.at[g], recv_sem=recv_sems.at[i],
            device_id=DEV[to], device_id_type=MESH).start()

    def need(*keys):
        for key in keys:
            if key not in waited:
                waited.add(key)
                ref, to, i = landing[key]
                pltpu.make_async_remote_copy(
                    src_ref=ref, dst_ref=ref, send_sem=send_sems.at[0], recv_sem=recv_sems.at[i],
                    device_id=DEV[to], device_id_type=MESH).wait_recv()

    def all_sent(group, ref):
        pltpu.make_async_remote_copy(
            src_ref=ref, dst_ref=ref, send_sem=send_sems.at[groups.pop(group)], recv_sem=recv_sems.at[0],
            device_id=DEV["pair"], device_id_type=MESH).wait_send()

    load_tok = pltpu.make_async_copy(tok_hbm, tok, local_sems.at[2])
    load_tok.start()
    vectors = [
        pltpu.make_async_copy(src, dst, local_sems.at[4 + i])
        for i, (src, dst) in enumerate(((gain_hbm, gain), (b1_hbm, b1), (b2_hbm, b2_own)))]
    for copy in vectors:
        copy.start()
    load1 = pltpu.make_async_copy(w1_hbm, w1.at[pl.ds(0, kb)], local_sems.at[0])
    load1.start()
    barrier = pltpu.get_barrier_semaphore()
    for to in DEV:
        pl.semaphore_signal(barrier, inc=1, device_id=DEV[to], device_id_type=MESH)

    C2 = kb // 3
    load2 = pltpu.make_async_copy(w2_hbm, w2.at[0], local_sems.at[1])
    CHUNKS = [(1, c) for c in range(len(W1_CHUNKS))] + [(2, c) for c in range(NW2)]

    def split(which, c):
        return W1_CHUNKS[c][2] if which == 1 else 4

    def part(which, c, ref, owner_grp, base=0):
        n = split(which, c)
        owner = owner_grp if n == 4 else owner_grp % 2
        if which == 1:
            c0, width1, _ = W1_CHUNKS[c]
            size, cols = kb // n, pl.ds(c0 * C1, width1 * C1)
        else:
            size, cols = nf // n, pl.ds(c * (kb // NW2), kb // NW2)
        return ref.at[pl.ds(pl.multiple_of(base + owner * size, 32), size), cols]

    def far_part(which, c, owner):
        return part(which, c, w1, owner, kb) if which == 1 else part(which, c, w2.at[1], owner)

    def send_weights():
        for which, c in CHUNKS:
            src = part(which, c, w1_hbm if which == 1 else w2_hbm, grp)
            send(("wy", which, c), src, far_part(which, c, grp), "far", group=(which, split(which, c)))
        send(("b2",), b2_hbm, b2_far, "far")
        load2.start()

    def w_y(which, c):
        mine = far_part(which, c, grp)
        group = (which, split(which, c))
        need(("wy", which, c))
        if group[1] == 4:
            send(("wt", which, c), mine, mine, "twin", far_part(which, c, twin_grp), group)
        send(("wc", which, c), mine, mine, "core", far_part(which, c, core_grp), group)

    def w_t(which, c):
        theirs = far_part(which, c, twin_grp)
        need(("wt", which, c))
        send(("wd", which, c), theirs, theirs, "core", far_part(which, c, diag_grp), (which, 4))

    def w_all(which, c):
        need(("wy", which, c), ("wc", which, c))
        if split(which, c) == 4:
            need(("wt", which, c), ("wd", which, c))

    def half_rows(mi):
        return pl.ds(pl.multiple_of(mi * tq, tq), tq)

    def norm(q):
        rows = pl.ds(q * tq, tq)
        total = jnp.zeros((tq, 1), F32)
        for b in range(nx):
            total += jnp.sum(tok[rows, pl.ds(b * kb, kb)].astype(F32), axis=1, keepdims=True)
        mean = total / width
        sq = jnp.zeros((tq, 1), F32)
        for b in range(nx):
            d = tok[rows, pl.ds(b * kb, kb)].astype(F32) - mean
            sq += jnp.sum(d * d, axis=1, keepdims=True)
        scale = lax.rsqrt(sq / width + 1e-06)

        def normed(block):
            g = gain[lanes(block)].reshape(1, kb)
            return ((tok[rows, lanes(block)].astype(F32) - mean) * scale * g).astype(BF16)

        for i, block in enumerate(pair_blocks):
            nb[rows, pl.ds(i * kb, kb)] = normed(block)
        for i, block in enumerate(my_blocks):
            x[OWN, q, 0, half_rows(m), pl.ds(i * kb, kb)] = normed(block)

    def ag_y(q):
        there = x.at[OWN, q, 0, half_rows(m)]
        send(("a2a", q), nb.at[pl.ds(q * tq, tq)], there, "pair", x.at[OWN, q, 0, half_rows(1 - m)])

    def ag_rows(q, r):
        send(("agu0", q), x.at[OWN, q, 0, r], x.at[DOWN, q, 0, r], "up", x.at[DOWN, q, 0], "ag")
        send(("agd0", q), x.at[OWN, q, 0, r], x.at[UP, q, 0, r], "dn", x.at[UP, q, 0], "ag")

    def ag_x00(q):
        ag_rows(q, half_rows(m))

    def ag_z(q):
        need(("a2a", q))
        send(("agz", q), x.at[OWN, q, 0], x.at[OWN, q, 1], "z")

    def ag_x0(q):
        need(("a2a", q))
        ag_rows(q, half_rows(1 - m))

    def ag_x1(q):
        need(("agz", q))
        send(("agu1", q), x.at[OWN, q, 1], x.at[DOWN, q, 1], "up", group="ag")
        send(("agd1", q), x.at[OWN, q, 1], x.at[UP, q, 1], "dn", group="ag")

    def ag_fu(q):
        need(("agu0", q))
        send(("agf", q), x.at[DOWN, q, 0], x.at[FAR, q, 0], "up", x.at[FAR, q])

    def ag_fd(q):
        need(("agd1", q))
        send(("agf", q), x.at[UP, q, 1], x.at[FAR, q, 1], "dn", x.at[FAR, q])

    SOURCES = {
        (OWN, 0): "a2a", (OWN, 1): "agz", (UP, 0): "agd0", (UP, 1): "agd1",
        (DOWN, 0): "agu0", (DOWN, 1): "agu1", (FAR, 0): "agf", (FAR, 1): "agf",
    }

    def at(ref, unit, cols):
        (xa, xb), (qa, qb), (za, zb) = unit
        return ref.at[pl.ds(xa, xb - xa), pl.ds(qa, qb - qa), pl.ds(za, zb - za), :, cols]

    def blocks(unit):
        (xa, xb), (qa, qb), (za, zb) = unit
        return [(i, j, k) for i in range(xa, xb) for j in range(qa, qb) for k in range(za, zb)]

    def shape_of(unit):
        (xa, xb), (qa, qb), (za, zb) = unit
        return (xb - xa, qb - qa, zb - za, 2 * tq)

    def flat(ref, unit):
        v = at(ref, unit, slice(None))[...]
        return v.reshape(-1, v.shape[-1])

    def mm1(unit, c0, n):
        if not waited & {"w1"}:
            waited.add("w1")
            load1.wait()
        for i, j, k in blocks(unit):
            need((SOURCES[i, k], j))
        for c, (first, count, _) in enumerate(W1_CHUNKS):
            if first < c0 + n and c0 < first + count:
                w_all(1, c)
        wide = C1 * (2 - n % 2)

        @pl.loop(0, n * C1 // wide)
        def _(c):
            cols = pl.ds(pl.multiple_of(c0 * C1 + c * wide, C1), wide)
            acc = jnp.dot(flat(x, unit), w1[:, cols], preferred_element_type=F32)
            acc = acc.reshape(shape_of(unit) + (wide,))
            at(p32, unit, cols)[...] = acc
            at(ps, unit, cols)[...] = acc.astype(BF16)

        cols = pl.ds(c0 * C1, n * C1)
        send(("p", unit, c0), at(ps, unit, cols), at(pr, unit, cols), "pair")

    def act(unit, c0, n):
        need(("p", unit, c0))

        @pl.loop(c0, c0 + n)
        def _(c):
            cols = pl.ds(pl.multiple_of(c * C1, C1), C1)
            bias = b1[cols].reshape(1, C1)
            for i, j, k in blocks(unit):
                v = p32[i, j, k, :, cols] + pr[i, j, k, :, cols].astype(F32) + bias
                hid[i, j, k, :, cols] = (0.5 * v * (1.0 + lax.erf(v * SQRT_HALF))).astype(BF16)

    def mm2(unit, h):
        if not waited & {"w2"}:
            waited.add("w2")
            load2.wait()
        if h:
            for c in range(NW2):
                w_all(2, c)

        @pl.loop(0, 3)
        def _(c):
            cols = pl.ds(pl.multiple_of(c * C2, 128), C2)
            acc = jnp.dot(flat(hid, unit), w2[h, :, cols], preferred_element_type=F32)
            at(os_.at[h], unit, cols)[...] = acc.reshape(shape_of(unit) + (C2,)).astype(BF16)

    def rs1(q, h):
        send(("r1", q, h), os_.at[h, FAR, q, 0], r1.at[h, q, 0], "up", r1.at[h, q])
        send(("r1", q, h), os_.at[h, FAR, q, 1], r1.at[h, q, 1], "dn", r1.at[h, q])

    def r2_send(q, h, x_pos, z_pos, to):
        d = 0 if to == "up" else 1
        send(("r2", q, h, z_pos), os_.at[h, x_pos, q, z_pos], r2.at[h, q, z_pos, d], to, r2.at[h, q, z_pos])

    def rs1n(q, h):
        r2_send(q, h, UP, 1, "up")

    def rs2(q, h):
        need(("r1", q, h))
        os_[h, UP, q, 0] = (os_[h, UP, q, 0].astype(F32) + r1[h, q, 0].astype(F32)).astype(BF16)
        r2_send(q, h, UP, 0, "up")
        os_[h, DOWN, q, 1] = (os_[h, DOWN, q, 1].astype(F32) + r1[h, q, 1].astype(F32)).astype(BF16)
        r2_send(q, h, DOWN, 1, "dn")
        r2_send(q, h, DOWN, 0, "dn")

    def rs3(q, h):
        need(("r2", q, h, 1))
        s = os_[h, OWN, q, 1].astype(F32) + r2[h, q, 1, 0].astype(F32) + r2[h, q, 1, 1].astype(F32)
        zs[h, q] = s.astype(BF16)
        send(("rz", q, h), zs.at[h, q], zr.at[h, q], "z")

    def rs4(q, h):
        rows = pl.ds(q * tq, tq)
        need(("r2", q, h, 0), ("rz", q, h))
        if h:
            need(("b2",))
        bias = (b2_far if h else b2_own)[...].reshape(1, kb)

        def branch(mi):
            r = half_rows(mi)
            s = os_[h, OWN, q, 0, r].astype(F32) + r2[h, q, 0, 0, r].astype(F32) + r2[h, q, 0, 1, r].astype(F32)
            return (s + zr[h, q, r].astype(F32) + bias).astype(BF16)

        fs[h, rows, :] = branch(1 - m)
        there = out.at[rows, lanes(my_blocks[h])]
        send(("f",), fs.at[h, rows], there, "pair", fs)
        fr[h, rows, :] = branch(m)
        pltpu.make_async_copy(fr.at[h, rows], there, local_sems.at[3]).start()

    order = [
        (ag_y, 0), (ag_x00, 3), (ag_y, 3), (ag_x00, 1), (ag_y, 1), (ag_z, 0), (ag_x00, 0), (ag_x0, 0), (ag_z, 1),
        (w_y, 1, 0), (ag_y, 2), (ag_x0, 1), (w_y, 1, 1), (ag_x1, 0), (ag_z, 2), (mm1, OWN01, 0, 1), (ag_fu, 0), (ag_x1, 1),
        (ag_fu, 1), (ag_z, 3), (w_t, 1, 1), (w_y, 1, 2), (mm1, NEAR0, 0, 1), (ag_fd, 0), (mm1, NEAR0, 1, 1),
        (mm1, OWN01, 1, 1), (ag_fd, 1), (mm1, NEAR0, 2, 2), (w_y, 1, 3), (mm1, OWN01, 2, 2), (mm1, FAR0, 1, 1),
        (mm1, OWN23, 0, 1), (mm1, OWN23, 2, 2), (ag_x00, 2), (mm1, FAR0, 0, 1), (mm1, OWN23, 1, 1), (ag_x0, 3),
        (mm1, REST1, 0, 4), (w_y, 1, 4), (ag_x0, 2), (ag_x1, 2), (w_t, 1, 3), (w_y, 1, 5), (mm1, REST1, 4, 4),
        (mm1, NEAR0, 4, 2), (ag_x1, 3), (w_y, 1, 6), (mm1, FAR0, 2, 2), (w_y, 2, 0), (mm1, FAR0, 6, 2), (w_t, 1, 5),
        (w_y, 2, 1), (ag_fd, 2), (act, OWN01, 1, 1), (ag_fu, 3), (ag_fd, 3), (mm1, NEAR0, 6, 2), (mm1, NEAR0, 8, 2),
        (w_t, 1, 6), (mm1, FAR0, 8, 2), (ag_fu, 2), (mm1, FAR0, 4, 2), (w_y, 2, 2), (act, FAR0, 1, 1), (w_y, 2, 3),
        (act, FAR0, 2, 2), (mm1, REST1, 8, 4), (mm1, NEAR0, 10, 2), (act, FAR0, 0, 1), (act, FAR0, 6, 2),
        (act, REST1, 0, 4), (act, NEAR0, 4, 2), (act, NEAR0, 1, 1), (w_y, 2, 4), (mm1, FAR0, 10, 2), (act, OWN01, 2, 2),
        (mm1, REST2, 6, 6), (act, NEAR0, 8, 2), (w_y, 2, 5), (w_y, 2, 6), (act, REST1, 4, 4), (act, FAR0, 4, 2),
        (mm1, REST2, 0, 6), (act, NEAR0, 6, 2), (act, FAR0, 8, 2), (act, NEAR0, 2, 2), (act, REST1, 8, 4), (w_t, 2, 4),
        (w_y, 2, 7), (mm2, REST1, 0), (act, NEAR0, 10, 2), (rs1, 1, 0), (act, NEAR0, 0, 1), (act, FAR0, 10, 2),
        (mm1, OWN01, 10, 2), (w_y, 2, 8), (w_t, 2, 3), (mm2, REST0, 0), (rs1, 0, 0), (rs1n, 1, 0), (w_t, 2, 0),
        (mm1, OWN01, 8, 2), (w_t, 2, 1), (w_t, 2, 5), (act, OWN23, 2, 2), (rs2, 1, 0), (w_t, 2, 7), (rs2, 0, 0),
        (w_t, 2, 6), (w_t, 2, 2), (act, OWN23, 0, 1), (act, OWN01, 0, 1), (rs1n, 0, 0), (mm1, OWN01, 6, 2), (w_t, 2, 8),
        (mm1, FAR3, 0, 12), (mm2, REST1, 1), (act, REST2, 6, 6), (rs1, 1, 1), (mm2, REST0, 1), (rs1, 0, 1),
        (act, REST2, 0, 6), (mm2, REST2, 0), (rs1, 2, 0), (mm2, REST2, 1), (rs1n, 0, 1), (rs2, 1, 1), (rs1, 2, 1),
        (mm1, OWN01, 4, 2), (rs2, 0, 1), (mm1, NEAR3, 0, 6), (mm1, NEAR3, 6, 6), (rs1n, 1, 1), (mm1, OWN23Z1, 4, 8),
        (rs1n, 2, 0), (act, OWN01, 10, 2), (act, OWN01, 6, 2), (act, FAR3, 0, 12), (mm2, FAR3, 1), (mm2, FAR3, 0),
        (rs1, 3, 1), (rs1, 3, 0), (act, OWN01, 4, 2), (mm1, OWN23Z0, 8, 4), (act, OWN01, 8, 2), (rs2, 2, 1),
        (mm1, OWN23Z0, 4, 4), (rs1n, 2, 1), (mm2, OWN01, 0), (rs3, 0, 0), (rs3, 1, 0), (act, OWN23, 1, 1), (rs2, 2, 0),
        (mm2, OWN01, 1), (rs3, 0, 1), (rs3, 1, 1), (rs4, 0, 0), (act, NEAR3, 0, 6), (act, NEAR3, 6, 6), (mm2, NEAR3, 1),
        (rs1n, 3, 1), (rs2, 3, 1), (rs4, 1, 0), (mm2, NEAR3, 0), (rs4, 0, 1), (act, OWN23Z1, 4, 8), (rs1n, 3, 0),
        (mm2, OWN23Z1, 1), (rs2, 3, 0), (rs4, 1, 1), (rs3, 2, 1), (rs3, 3, 1), (mm2, OWN23Z1, 0), (act, OWN23Z0, 8, 4),
        (act, OWN23Z0, 4, 4), (rs3, 2, 0), (rs3, 3, 0), (mm2, OWN23Z0, 1), (rs4, 3, 1), (rs4, 2, 1), (mm2, OWN23Z0, 0),
        (rs4, 2, 0), (rs4, 3, 0),
    ]
    for copy in [load_tok] + vectors:
        copy.wait()
    for q in range(NQ):
        norm(q)
    pl.semaphore_wait(barrier, len(DEV))
    send_weights()
    for step, *args in order:
        step(*args)
    need(("f",))
    pltpu.make_async_copy(fr, fr, local_sems.at[3]).wait()
    wide = {n: C1 * sum(count for _, count, split_in in W1_CHUNKS if split_in == n) for n in (2, 4)}
    for group, ref in (
        ("a2a", nb), ("ag", x.at[pl.ds(0, 2)]), ("agf", x.at[FAR]), ("agz", x.at[OWN, :, 1]), ("b2", b2_far),
        ((1, 2), w1.at[pl.ds(0, kb), pl.ds(0, wide[2])]), ((1, 4), w1.at[pl.ds(0, kb), pl.ds(0, wide[4])]), ((2, 4), w2.at[1]),
        ("p", ps), ("r1", r1), ("r2", r2), ("rz", zs), ("f", fs),
    ):
        all_sent(group, ref)
    assert waited >= set(ids) and not groups
    assert len(ids) <= N_RECV, len(ids)


def local(tokens, ln_gain, w_in, b_in, w_out, b_out):
    n_tok, d = tokens.shape
    kb, nf = w_in.shape
    tq = n_tok // NQ
    pz = 2 * tq
    tiles = (4, NQ, 2, pz)
    vm = pltpu.VMEM
    flops = 4 * 16 * n_tok * 2 * kb * nf
    branch = pl.pallas_call(
        functools.partial(kernel, (tq, kb, nf)),
        out_shape=jax.ShapeDtypeStruct((n_tok, d), BF16),
        in_specs=[pl.BlockSpec(memory_space=pltpu.HBM)] * 6,
        out_specs=pl.BlockSpec(memory_space=pl.ANY),
        scratch_shapes=[
            vm((n_tok, d), BF16),
            vm((d,), F32),
            vm((nf,), F32),
            vm((kb,), F32),
            vm((2 * kb, nf), BF16),
            vm((2, nf, kb), BF16),
            vm(tiles + (2 * kb,), BF16),
            vm((n_tok, 2 * kb), BF16),
            vm(tiles + (nf,), F32),
            vm(tiles + (nf,), BF16),
            vm(tiles + (nf,), BF16),
            vm(tiles + (nf,), BF16),
            vm((2,) + tiles + (kb,), BF16),
            vm((2, NQ, 2, pz, kb), BF16),
            vm((2, NQ, 2, 2, pz, kb), BF16),
            vm((2, NQ, pz, kb), BF16),
            vm((2, NQ, pz, kb), BF16),
            vm((2, n_tok, kb), BF16),
            vm((2, n_tok, kb), BF16),
            vm((kb,), F32),
            pltpu.SemaphoreType.DMA((13,)),
            pltpu.SemaphoreType.DMA((N_RECV,)),
            pltpu.SemaphoreType.DMA((7,)),
        ],
        compiler_params=pltpu.CompilerParams(
            collective_id=0, has_side_effects=True, vmem_limit_bytes=52 * 2**20),
        cost_estimate=pl.CostEstimate(flops=flops, bytes_accessed=4 * kb * nf, transcendentals=0),
    )(*[pltpu.with_memory_space_constraint(a, pltpu.HBM) for a in (tokens, ln_gain, w_in, b_in, w_out, b_out)])
    return (tokens.astype(F32) + branch.astype(F32)).astype(BF16)


def solution(mesh):
    tokens = P(("grp", "row", "col"), None)
    return jax.shard_map(
        local,
        mesh=mesh,
        in_specs=(tokens, P(), P("row", "col"), P("col"), P("col", "row"), P("row")),
        out_specs=tokens,
        check_vma=False,
    )
```

profile of v0, /device:TPU:0, one launch (start us, length us, event | category | flops | bytes accessed | tf_op | source)
XLA Modules:
  0.0 103.9 jit_solution(9294706448070621571)
XLA Ops:
  0.0 0.0 copy-start
  0.0 103.0 %shard_map.64 = bf16[64,4608]{1,0:T(8,128)(2,1)S(1)} custom-call(bf16[64,4608]{1,0:T(8,128)(2,1)} %tok_hbm.1, f32[4608]{0:T(1024)} %gain_hbm.1, bf16[1152,1536]{1,0:T(8,128)(2,1)} %w1_hbm.1, f32[1536]{0:T(1024)} %b1_hbm.1, bf16[1536,1152]{1,0:T(8,128)(2,1)} %w2_hbm.1, f32[1152]{0:T(1024)} %b2_hbm.1), custom_call_target="tpu_custom_call" | custom-call | flops 14495514624 | bytes 7077888 | tf_op jit(solution)/shard_map/pallas_call | solution.py:365
  103.0 0.0 copy-done
  103.0 1.0 add_convert_fusion
Async XLA Ops:
  0.0 103.0 %copy-start = (bf16[64,4608]{1,0:T(8,128)(2,1)S(1)}, bf16[64,4608]{1,0:T(8,128)(2,1)}, u32[]{:S(2)}) copy-start(bf16[64,4608]{1,0:T(8,128)(2,1)} %tok_hbm.1) | copy-start | bytes 1769476
where the time goes:
time: 104 us
  Pallas kernels  103 us (99%)
    pallas_call x1, Pallas kernels, local(): pl.pallas_call(functools.partial(kernel, (tq, kb, nf)), out_shape=jax.Sha...  103 us

commit v1 on v0

--- a/solution.py
+++ b/solution.py
@@ -10,21 +10,21 @@
 MESH = pl.DeviceIdType.MESH
 F32, BF16 = jnp.float32, jnp.bfloat16
 NQ = 4
-N_RECV = 155
+N_RECV = 158
 SQRT_HALF = 0.7071067811865476
 OWN, UP, DOWN, FAR = 0, 1, 2, 3
 C1 = 128
-W1_CHUNKS = ((0, 1, 2), (1, 1, 4), (2, 2, 2), (4, 2, 4), (6, 2, 2), (8, 2, 4), (10, 2, 4))
+W1_CHUNKS = ((0, 2, 4), (2, 2, 2), (4, 2, 4), (6, 2, 2), (8, 2, 4), (10, 2, 4))
 NW2 = 9
 Z = (0, 2)
 OWN01, NEAR0, FAR0 = ((0, 1), (0, 2), Z), ((1, 3), (0, 1), Z), ((3, 4), (0, 1), Z)
 REST0, REST1, REST2 = ((1, 4), (0, 1), Z), ((1, 4), (1, 2), Z), ((1, 4), (2, 3), Z)
-NEAR3, FAR3 = ((1, 3), (3, 4), Z), ((3, 4), (3, 4), Z)
+NEAR3Z1, NEAR3Z0, FAR3 = ((1, 3), (3, 4), (1, 2)), ((1, 3), (3, 4), (0, 1)), ((3, 4), (3, 4), Z)
 OWN23, OWN23Z1, OWN23Z0 = ((0, 1), (2, 4), Z), ((0, 1), (2, 4), (1, 2)), ((0, 1), (2, 4), (0, 1))
 
 
 def kernel(dims, tok_hbm, gain_hbm, w1_hbm, b1_hbm, w2_hbm, b2_hbm, out,
-           tok, gain, b1, b2_own, w1, w2, x, nb, p32, ps, pr, hid, os_, r1, r2, zs, zr, fs, fr, b2_far,
+           tok, gain, b1, b2_own, w1, w2, x, nb, p32, ps, pr, hid, os_, r1, r2, rf, zs, zr, fs, fr, b2_far,
            send_sems, recv_sems, local_sems):
     tq, kb, nf = dims
     nx = 4
@@ -260,24 +260,34 @@
             acc = jnp.dot(flat(hid, unit), w2[h, :, cols], preferred_element_type=F32)
             at(os_.at[h], unit, cols)[...] = acc.reshape(shape_of(unit) + (C2,)).astype(BF16)
 
+    def add_to(ref, more):
+        ref[...] = (ref[...].astype(F32) + more.astype(F32)).astype(BF16)
+
+    def r2_send(q, h, d, z_pos):
+        src = os_.at[h, UP + d, q, z_pos]
+        send(("r2", q, h, z_pos), src, r2.at[h, q, z_pos, d], ("up", "dn")[d], r2.at[h, q, z_pos])
+
+    def rsz(q, h):
+        send(("rf", q, h), os_.at[h, FAR, q, 1], rf.at[h, q], "z")
+
     def rs1(q, h):
-        send(("r1", q, h), os_.at[h, FAR, q, 0], r1.at[h, q, 0], "up", r1.at[h, q])
-        send(("r1", q, h), os_.at[h, FAR, q, 1], r1.at[h, q, 1], "dn", r1.at[h, q])
-
-    def r2_send(q, h, x_pos, z_pos, to):
-        d = 0 if to == "up" else 1
-        send(("r2", q, h, z_pos), os_.at[h, x_pos, q, z_pos], r2.at[h, q, z_pos, d], to, r2.at[h, q, z_pos])
+        need(("rf", q, h))
+        add_to(os_.at[h, FAR, q, 0], rf[h, q])
+        send(("r1", q, h), os_.at[h, FAR, q, 0], r1.at[h, q], ("up", "dn")[q % 2])
 
     def rs1n(q, h):
-        r2_send(q, h, UP, 1, "up")
+        d = q % 2
+        r2_send(q, h, d, 1)
+        r2_send(q, h, 1 - d, 1)
+
+    def rs1o(q, h):
+        r2_send(q, h, 1 - q % 2, 0)
 
     def rs2(q, h):
+        d = q % 2
         need(("r1", q, h))
-        os_[h, UP, q, 0] = (os_[h, UP, q, 0].astype(F32) + r1[h, q, 0].astype(F32)).astype(BF16)
-        r2_send(q, h, UP, 0, "up")
-        os_[h, DOWN, q, 1] = (os_[h, DOWN, q, 1].astype(F32) + r1[h, q, 1].astype(F32)).astype(BF16)
-        r2_send(q, h, DOWN, 1, "dn")
-        r2_send(q, h, DOWN, 0, "dn")
+        add_to(os_.at[h, UP + d, q, 0], r1[h, q])
+        r2_send(q, h, d, 0)
 
     def rs3(q, h):
         need(("r2", q, h, 1))
@@ -304,34 +314,35 @@
         pltpu.make_async_copy(fr.at[h, rows], there, local_sems.at[3]).start()
 
     order = [
-        (ag_y, 0), (ag_x00, 3), (ag_y, 3), (ag_x00, 1), (ag_y, 1), (ag_z, 0), (ag_x00, 0), (ag_x0, 0), (ag_z, 1),
-        (w_y, 1, 0), (ag_y, 2), (ag_x0, 1), (w_y, 1, 1), (ag_x1, 0), (ag_z, 2), (mm1, OWN01, 0, 1), (ag_fu, 0), (ag_x1, 1),
-        (ag_fu, 1), (ag_z, 3), (w_t, 1, 1), (w_y, 1, 2), (mm1, NEAR0, 0, 1), (ag_fd, 0), (mm1, NEAR0, 1, 1),
-        (mm1, OWN01, 1, 1), (ag_fd, 1), (mm1, NEAR0, 2, 2), (w_y, 1, 3), (mm1, OWN01, 2, 2), (mm1, FAR0, 1, 1),
-        (mm1, OWN23, 0, 1), (mm1, OWN23, 2, 2), (ag_x00, 2), (mm1, FAR0, 0, 1), (mm1, OWN23, 1, 1), (ag_x0, 3),
-        (mm1, REST1, 0, 4), (w_y, 1, 4), (ag_x0, 2), (ag_x1, 2), (w_t, 1, 3), (w_y, 1, 5), (mm1, REST1, 4, 4),
-        (mm1, NEAR0, 4, 2), (ag_x1, 3), (w_y, 1, 6), (mm1, FAR0, 2, 2), (w_y, 2, 0), (mm1, FAR0, 6, 2), (w_t, 1, 5),
-        (w_y, 2, 1), (ag_fd, 2), (act, OWN01, 1, 1), (ag_fu, 3), (ag_fd, 3), (mm1, NEAR0, 6, 2), (mm1, NEAR0, 8, 2),
-        (w_t, 1, 6), (mm1, FAR0, 8, 2), (ag_fu, 2), (mm1, FAR0, 4, 2), (w_y, 2, 2), (act, FAR0, 1, 1), (w_y, 2, 3),
-        (act, FAR0, 2, 2), (mm1, REST1, 8, 4), (mm1, NEAR0, 10, 2), (act, FAR0, 0, 1), (act, FAR0, 6, 2),
-        (act, REST1, 0, 4), (act, NEAR0, 4, 2), (act, NEAR0, 1, 1), (w_y, 2, 4), (mm1, FAR0, 10, 2), (act, OWN01, 2, 2),
-        (mm1, REST2, 6, 6), (act, NEAR0, 8, 2), (w_y, 2, 5), (w_y, 2, 6), (act, REST1, 4, 4), (act, FAR0, 4, 2),
-        (mm1, REST2, 0, 6), (act, NEAR0, 6, 2), (act, FAR0, 8, 2), (act, NEAR0, 2, 2), (act, REST1, 8, 4), (w_t, 2, 4),
-        (w_y, 2, 7), (mm2, REST1, 0), (act, NEAR0, 10, 2), (rs1, 1, 0), (act, NEAR0, 0, 1), (act, FAR0, 10, 2),
-        (mm1, OWN01, 10, 2), (w_y, 2, 8), (w_t, 2, 3), (mm2, REST0, 0), (rs1, 0, 0), (rs1n, 1, 0), (w_t, 2, 0),
-        (mm1, OWN01, 8, 2), (w_t, 2, 1), (w_t, 2, 5), (act, OWN23, 2, 2), (rs2, 1, 0), (w_t, 2, 7), (rs2, 0, 0),
-        (w_t, 2, 6), (w_t, 2, 2), (act, OWN23, 0, 1), (act, OWN01, 0, 1), (rs1n, 0, 0), (mm1, OWN01, 6, 2), (w_t, 2, 8),
-        (mm1, FAR3, 0, 12), (mm2, REST1, 1), (act, REST2, 6, 6), (rs1, 1, 1), (mm2, REST0, 1), (rs1, 0, 1),
-        (act, REST2, 0, 6), (mm2, REST2, 0), (rs1, 2, 0), (mm2, REST2, 1), (rs1n, 0, 1), (rs2, 1, 1), (rs1, 2, 1),
-        (mm1, OWN01, 4, 2), (rs2, 0, 1), (mm1, NEAR3, 0, 6), (mm1, NEAR3, 6, 6), (rs1n, 1, 1), (mm1, OWN23Z1, 4, 8),
-        (rs1n, 2, 0), (act, OWN01, 10, 2), (act, OWN01, 6, 2), (act, FAR3, 0, 12), (mm2, FAR3, 1), (mm2, FAR3, 0),
-        (rs1, 3, 1), (rs1, 3, 0), (act, OWN01, 4, 2), (mm1, OWN23Z0, 8, 4), (act, OWN01, 8, 2), (rs2, 2, 1),
-        (mm1, OWN23Z0, 4, 4), (rs1n, 2, 1), (mm2, OWN01, 0), (rs3, 0, 0), (rs3, 1, 0), (act, OWN23, 1, 1), (rs2, 2, 0),
-        (mm2, OWN01, 1), (rs3, 0, 1), (rs3, 1, 1), (rs4, 0, 0), (act, NEAR3, 0, 6), (act, NEAR3, 6, 6), (mm2, NEAR3, 1),
-        (rs1n, 3, 1), (rs2, 3, 1), (rs4, 1, 0), (mm2, NEAR3, 0), (rs4, 0, 1), (act, OWN23Z1, 4, 8), (rs1n, 3, 0),
-        (mm2, OWN23Z1, 1), (rs2, 3, 0), (rs4, 1, 1), (rs3, 2, 1), (rs3, 3, 1), (mm2, OWN23Z1, 0), (act, OWN23Z0, 8, 4),
-        (act, OWN23Z0, 4, 4), (rs3, 2, 0), (rs3, 3, 0), (mm2, OWN23Z0, 1), (rs4, 3, 1), (rs4, 2, 1), (mm2, OWN23Z0, 0),
-        (rs4, 2, 0), (rs4, 3, 0),
+        (ag_y, 0), (ag_x00, 2), (ag_y, 1), (ag_y, 3), (ag_z, 0), (ag_x00, 0), (ag_y, 2), (ag_x0, 0), (w_y, 1, 0), (ag_z, 1),
+        (ag_x00, 1), (ag_x1, 0), (w_t, 1, 0), (ag_fu, 0), (ag_z, 2), (ag_x0, 1), (ag_z, 3), (ag_fd, 0), (ag_x1, 1),
+        (w_y, 1, 1), (mm1, NEAR0, 0, 2), (w_y, 1, 2), (ag_x00, 3), (mm1, OWN01, 0, 2), (mm1, NEAR0, 2, 2), (ag_fu, 1),
+        (mm1, FAR0, 2, 2), (mm1, OWN01, 2, 2), (mm1, OWN23, 0, 2), (mm1, OWN23, 2, 2), (w_y, 1, 3), (ag_fd, 1),
+        (mm1, FAR0, 0, 2), (mm1, FAR0, 6, 2), (w_t, 1, 2), (ag_x1, 3), (ag_x1, 2), (w_y, 1, 4), (ag_x0, 3),
+        (mm1, OWN01, 6, 2), (mm1, NEAR0, 6, 2), (ag_x0, 2), (mm1, REST1, 0, 4), (w_y, 1, 5), (w_t, 1, 4), (w_y, 2, 0),
+        (mm1, REST1, 4, 4), (w_y, 2, 2), (w_t, 1, 5), (act, NEAR0, 2, 2), (mm1, NEAR0, 4, 2), (w_y, 2, 1),
+        (mm1, FAR0, 8, 2), (ag_fu, 2), (ag_fd, 2), (w_y, 2, 3), (mm1, REST1, 8, 4), (mm1, NEAR0, 8, 2), (w_y, 2, 5),
+        (act, FAR0, 6, 2), (ag_fu, 3), (ag_fd, 3), (mm1, FAR0, 10, 2), (w_y, 2, 4), (act, REST1, 4, 4), (mm1, NEAR0, 10, 2),
+        (act, REST1, 0, 4), (mm1, FAR0, 4, 2), (mm1, REST2, 6, 6), (w_y, 2, 6), (mm1, REST2, 0, 6), (act, REST1, 8, 4),
+        (w_y, 2, 7), (mm1, FAR3, 0, 12), (w_y, 2, 8), (w_t, 2, 1), (act, NEAR0, 0, 2), (act, OWN01, 6, 2), (w_t, 2, 0),
+        (act, FAR0, 10, 2), (w_t, 2, 3), (mm2, REST1, 0), (act, NEAR0, 8, 2), (act, FAR0, 2, 2), (mm1, OWN01, 8, 2),
+        (w_t, 2, 4), (w_t, 2, 6), (act, NEAR0, 6, 2), (w_t, 2, 5), (act, OWN01, 0, 2), (rs1n, 1, 0), (act, FAR0, 0, 2),
+        (rsz, 1, 0), (act, NEAR0, 4, 2), (act, FAR0, 4, 2), (act, OWN01, 2, 2), (act, FAR0, 8, 2), (mm1, OWN01, 10, 2),
+        (w_t, 2, 2), (act, NEAR0, 10, 2), (mm2, REST0, 0), (rs1n, 0, 0), (mm1, OWN01, 4, 2), (w_t, 2, 7), (w_t, 2, 8),
+        (rsz, 0, 0), (mm1, NEAR3Z1, 0, 12), (rs1o, 1, 0), (rs1, 1, 0), (mm2, REST0, 1), (rs1n, 0, 1), (rs1o, 0, 1),
+        (rs1, 0, 0), (rsz, 0, 1), (mm1, OWN23Z1, 4, 8), (mm2, REST1, 1), (rs1o, 0, 0), (rsz, 1, 1), (act, REST2, 6, 6),
+        (mm1, NEAR3Z0, 6, 6), (rs1n, 1, 1), (act, REST2, 0, 6), (mm2, REST2, 0), (rs1, 0, 1), (rs1o, 1, 1), (rsz, 2, 0),
+        (mm2, REST2, 1), (rs1n, 2, 0), (act, FAR3, 0, 12), (rsz, 2, 1), (rs1, 1, 1), (mm2, FAR3, 0), (rsz, 3, 0),
+        (act, OWN01, 8, 2), (rs2, 1, 0), (rs1n, 2, 1), (act, OWN23, 0, 2), (mm1, NEAR3Z0, 0, 6), (rs2, 0, 0),
+        (act, OWN23, 2, 2), (mm2, FAR3, 1), (rs1, 2, 0), (rsz, 3, 1), (act, OWN01, 10, 2), (rs1, 2, 1), (rs2, 0, 1),
+        (rs1o, 2, 0), (act, OWN01, 4, 2), (mm2, OWN01, 0), (rs3, 1, 0), (rs3, 0, 0), (mm2, OWN01, 1), (rs2, 1, 1),
+        (rs3, 1, 1), (mm1, OWN23Z0, 4, 4), (mm1, OWN23Z0, 8, 4), (rs3, 0, 1), (act, NEAR3Z1, 0, 12), (rs1, 3, 1),
+        (mm2, NEAR3Z1, 0), (rs1n, 3, 0), (rs4, 1, 0), (mm2, NEAR3Z1, 1), (rs4, 0, 0), (rs1, 3, 0), (rs2, 2, 0),
+        (act, OWN23Z1, 4, 8), (rs1n, 3, 1), (mm2, OWN23Z1, 1), (rs4, 1, 1), (rs3, 2, 1), (rs2, 2, 1), (rs1o, 2, 1),
+        (mm2, OWN23Z1, 0), (act, NEAR3Z0, 6, 6), (rs4, 0, 1), (rs3, 2, 0), (rs3, 3, 0), (act, NEAR3Z0, 0, 6),
+        (mm2, NEAR3Z0, 0), (rs2, 3, 0), (rs1o, 3, 0), (mm2, NEAR3Z0, 1), (act, OWN23Z0, 4, 4), (rs3, 3, 1), (rs1o, 3, 1),
+        (rs2, 3, 1), (act, OWN23Z0, 8, 4), (mm2, OWN23Z0, 1), (rs4, 2, 1), (mm2, OWN23Z0, 0), (rs4, 2, 0), (rs4, 3, 0),
+        (rs4, 3, 1),
     ]
     for copy in [load_tok] + vectors:
         copy.wait()
@@ -347,7 +358,7 @@
     for group, ref in (
         ("a2a", nb), ("ag", x.at[pl.ds(0, 2)]), ("agf", x.at[FAR]), ("agz", x.at[OWN, :, 1]), ("b2", b2_far),
         ((1, 2), w1.at[pl.ds(0, kb), pl.ds(0, wide[2])]), ((1, 4), w1.at[pl.ds(0, kb), pl.ds(0, wide[4])]), ((2, 4), w2.at[1]),
-        ("p", ps), ("r1", r1), ("r2", r2), ("rz", zs), ("f", fs),
+        ("p", ps), ("r1", r1), ("r2", r2), ("rf", rf), ("rz", zs), ("f", fs),
     ):
         all_sent(group, ref)
     assert waited >= set(ids) and not groups
@@ -381,14 +392,15 @@
             vm(tiles + (nf,), BF16),
             vm(tiles + (nf,), BF16),
             vm((2,) + tiles + (kb,), BF16),
-            vm((2, NQ, 2, pz, kb), BF16),
+            vm((2, NQ, pz, kb), BF16),
             vm((2, NQ, 2, 2, pz, kb), BF16),
+            vm((2, NQ, pz, kb), BF16),
             vm((2, NQ, pz, kb), BF16),
             vm((2, NQ, pz, kb), BF16),
             vm((2, n_tok, kb), BF16),
             vm((2, n_tok, kb), BF16),
             vm((kb,), F32),
-            pltpu.SemaphoreType.DMA((13,)),
+            pltpu.SemaphoreType.DMA((14,)),
             pltpu.SemaphoreType.DMA((N_RECV,)),
             pltpu.SemaphoreType.DMA((7,)),
         ],

time: 104 us -> 101 us (0.971)
  Pallas kernels: 103 us -> 99.9 us
    pallas_call x1, Pallas kernels: 103 us -> 99.9 us  [local(): pl.pallas_call(functools.partial(kernel, (tq, kb, nf)), out_shape=jax.Sha...]
where the time goes in v1:
time: 101 us
  Pallas kernels  99.9 us (99%)
    pallas_call x1, Pallas kernels, local(): pl.pallas_call(functools.partial(kernel, (tq, kb, nf)), out_shape=jax.Sha...  99.9 us

profile of v1, /device:TPU:0, one launch (start us, length us, event | category | flops | bytes accessed | tf_op | source)
XLA Modules:
  0.0 100.9 jit_solution(1688314825594123814)
XLA Ops:
  0.0 0.0 copy-start
  0.0 99.9 %shard_map.64 = bf16[64,4608]{1,0:T(8,128)(2,1)S(1)} custom-call(bf16[64,4608]{1,0:T(8,128)(2,1)} %tok_hbm.1, f32[4608]{0:T(1024)} %gain_hbm.1, bf16[1152,1536]{1,0:T(8,128)(2,1)} %w1_hbm.1, f32[1536]{0:T(1024)} %b1_hbm.1, bf16[1536,1152]{1,0:T(8,128)(2,1)} %w2_hbm.1, f32[1152]{0:T(1024)} %b2_hbm.1), custom_call_target="tpu_custom_call" | custom-call | flops 14495514624 | bytes 7077888 | tf_op jit(solution)/shard_map/pallas_call | solution.py:376
  99.9 0.0 copy-done
  99.9 1.0 add_convert_fusion
Async XLA Ops:
  0.0 99.9 %copy-start = (bf16[64,4608]{1,0:T(8,128)(2,1)S(1)}, bf16[64,4608]{1,0:T(8,128)(2,1)}, u32[]{:S(2)}) copy-start(bf16[64,4608]{1,0:T(8,128)(2,1)} %tok_hbm.1) | copy-start | bytes 1769476

commit v2 on v1

--- a/solution.py
+++ b/solution.py
@@ -314,35 +314,34 @@
         pltpu.make_async_copy(fr.at[h, rows], there, local_sems.at[3]).start()
 
     order = [
-        (ag_y, 0), (ag_x00, 2), (ag_y, 1), (ag_y, 3), (ag_z, 0), (ag_x00, 0), (ag_y, 2), (ag_x0, 0), (w_y, 1, 0), (ag_z, 1),
-        (ag_x00, 1), (ag_x1, 0), (w_t, 1, 0), (ag_fu, 0), (ag_z, 2), (ag_x0, 1), (ag_z, 3), (ag_fd, 0), (ag_x1, 1),
-        (w_y, 1, 1), (mm1, NEAR0, 0, 2), (w_y, 1, 2), (ag_x00, 3), (mm1, OWN01, 0, 2), (mm1, NEAR0, 2, 2), (ag_fu, 1),
-        (mm1, FAR0, 2, 2), (mm1, OWN01, 2, 2), (mm1, OWN23, 0, 2), (mm1, OWN23, 2, 2), (w_y, 1, 3), (ag_fd, 1),
-        (mm1, FAR0, 0, 2), (mm1, FAR0, 6, 2), (w_t, 1, 2), (ag_x1, 3), (ag_x1, 2), (w_y, 1, 4), (ag_x0, 3),
-        (mm1, OWN01, 6, 2), (mm1, NEAR0, 6, 2), (ag_x0, 2), (mm1, REST1, 0, 4), (w_y, 1, 5), (w_t, 1, 4), (w_y, 2, 0),
-        (mm1, REST1, 4, 4), (w_y, 2, 2), (w_t, 1, 5), (act, NEAR0, 2, 2), (mm1, NEAR0, 4, 2), (w_y, 2, 1),
-        (mm1, FAR0, 8, 2), (ag_fu, 2), (ag_fd, 2), (w_y, 2, 3), (mm1, REST1, 8, 4), (mm1, NEAR0, 8, 2), (w_y, 2, 5),
-        (act, FAR0, 6, 2), (ag_fu, 3), (ag_fd, 3), (mm1, FAR0, 10, 2), (w_y, 2, 4), (act, REST1, 4, 4), (mm1, NEAR0, 10, 2),
-        (act, REST1, 0, 4), (mm1, FAR0, 4, 2), (mm1, REST2, 6, 6), (w_y, 2, 6), (mm1, REST2, 0, 6), (act, REST1, 8, 4),
-        (w_y, 2, 7), (mm1, FAR3, 0, 12), (w_y, 2, 8), (w_t, 2, 1), (act, NEAR0, 0, 2), (act, OWN01, 6, 2), (w_t, 2, 0),
-        (act, FAR0, 10, 2), (w_t, 2, 3), (mm2, REST1, 0), (act, NEAR0, 8, 2), (act, FAR0, 2, 2), (mm1, OWN01, 8, 2),
-        (w_t, 2, 4), (w_t, 2, 6), (act, NEAR0, 6, 2), (w_t, 2, 5), (act, OWN01, 0, 2), (rs1n, 1, 0), (act, FAR0, 0, 2),
-        (rsz, 1, 0), (act, NEAR0, 4, 2), (act, FAR0, 4, 2), (act, OWN01, 2, 2), (act, FAR0, 8, 2), (mm1, OWN01, 10, 2),
-        (w_t, 2, 2), (act, NEAR0, 10, 2), (mm2, REST0, 0), (rs1n, 0, 0), (mm1, OWN01, 4, 2), (w_t, 2, 7), (w_t, 2, 8),
-        (rsz, 0, 0), (mm1, NEAR3Z1, 0, 12), (rs1o, 1, 0), (rs1, 1, 0), (mm2, REST0, 1), (rs1n, 0, 1), (rs1o, 0, 1),
-        (rs1, 0, 0), (rsz, 0, 1), (mm1, OWN23Z1, 4, 8), (mm2, REST1, 1), (rs1o, 0, 0), (rsz, 1, 1), (act, REST2, 6, 6),
-        (mm1, NEAR3Z0, 6, 6), (rs1n, 1, 1), (act, REST2, 0, 6), (mm2, REST2, 0), (rs1, 0, 1), (rs1o, 1, 1), (rsz, 2, 0),
-        (mm2, REST2, 1), (rs1n, 2, 0), (act, FAR3, 0, 12), (rsz, 2, 1), (rs1, 1, 1), (mm2, FAR3, 0), (rsz, 3, 0),
-        (act, OWN01, 8, 2), (rs2, 1, 0), (rs1n, 2, 1), (act, OWN23, 0, 2), (mm1, NEAR3Z0, 0, 6), (rs2, 0, 0),
-        (act, OWN23, 2, 2), (mm2, FAR3, 1), (rs1, 2, 0), (rsz, 3, 1), (act, OWN01, 10, 2), (rs1, 2, 1), (rs2, 0, 1),
-        (rs1o, 2, 0), (act, OWN01, 4, 2), (mm2, OWN01, 0), (rs3, 1, 0), (rs3, 0, 0), (mm2, OWN01, 1), (rs2, 1, 1),
-        (rs3, 1, 1), (mm1, OWN23Z0, 4, 4), (mm1, OWN23Z0, 8, 4), (rs3, 0, 1), (act, NEAR3Z1, 0, 12), (rs1, 3, 1),
-        (mm2, NEAR3Z1, 0), (rs1n, 3, 0), (rs4, 1, 0), (mm2, NEAR3Z1, 1), (rs4, 0, 0), (rs1, 3, 0), (rs2, 2, 0),
-        (act, OWN23Z1, 4, 8), (rs1n, 3, 1), (mm2, OWN23Z1, 1), (rs4, 1, 1), (rs3, 2, 1), (rs2, 2, 1), (rs1o, 2, 1),
-        (mm2, OWN23Z1, 0), (act, NEAR3Z0, 6, 6), (rs4, 0, 1), (rs3, 2, 0), (rs3, 3, 0), (act, NEAR3Z0, 0, 6),
-        (mm2, NEAR3Z0, 0), (rs2, 3, 0), (rs1o, 3, 0), (mm2, NEAR3Z0, 1), (act, OWN23Z0, 4, 4), (rs3, 3, 1), (rs1o, 3, 1),
-        (rs2, 3, 1), (act, OWN23Z0, 8, 4), (mm2, OWN23Z0, 1), (rs4, 2, 1), (mm2, OWN23Z0, 0), (rs4, 2, 0), (rs4, 3, 0),
-        (rs4, 3, 1),
+        (ag_y, 0), (ag_y, 1), (ag_x00, 0), (ag_y, 3), (ag_y, 2), (ag_x00, 3), (ag_z, 0), (w_y, 1, 0), (ag_z, 1), (ag_z, 3),
+        (ag_x00, 1), (ag_z, 2), (ag_x0, 0), (ag_x1, 0), (w_y, 1, 1), (ag_x0, 1), (w_t, 1, 0), (ag_x1, 1),
+        (mm1, OWN01, 2, 2), (ag_fd, 0), (w_y, 1, 2), (mm1, OWN01, 0, 2), (mm1, NEAR0, 2, 2), (ag_fu, 0), (mm1, NEAR0, 0, 2),
+        (ag_fd, 1), (mm1, OWN23, 0, 2), (ag_fu, 1), (w_y, 1, 3), (ag_x00, 2), (mm1, OWN23, 2, 2), (mm1, FAR0, 0, 2),
+        (ag_x0, 2), (mm1, FAR0, 2, 2), (w_y, 1, 4), (w_t, 1, 2), (mm1, FAR0, 6, 2), (mm1, NEAR0, 6, 2), (ag_x1, 2),
+        (mm1, OWN01, 6, 2), (w_y, 1, 5), (mm1, REST1, 0, 4), (ag_x0, 3), (w_y, 2, 0), (w_t, 1, 4), (w_y, 2, 1),
+        (mm1, REST1, 4, 4), (w_y, 2, 2), (ag_x1, 3), (act, NEAR0, 6, 2), (w_t, 1, 5), (w_y, 2, 3), (mm1, NEAR0, 8, 2),
+        (mm1, NEAR0, 4, 2), (ag_fu, 2), (act, NEAR0, 0, 2), (ag_fu, 3), (mm1, FAR0, 4, 2), (mm1, FAR0, 8, 2),
+        (act, NEAR0, 2, 2), (ag_fd, 2), (mm1, REST1, 8, 4), (w_y, 2, 5), (ag_fd, 3), (mm1, FAR0, 10, 2), (act, OWN01, 2, 2),
+        (act, REST1, 4, 4), (w_y, 2, 6), (mm1, NEAR0, 10, 2), (w_y, 2, 4), (mm1, REST2, 6, 6), (w_y, 2, 7),
+        (act, REST1, 0, 4), (mm1, REST2, 0, 6), (act, OWN23, 0, 2), (w_y, 2, 8), (mm1, FAR3, 0, 12), (act, REST1, 8, 4),
+        (w_t, 2, 0), (mm2, REST1, 0), (w_t, 2, 2), (act, FAR0, 10, 2), (act, FAR0, 4, 2), (act, NEAR0, 8, 2), (w_t, 2, 1),
+        (mm1, OWN01, 8, 2), (act, FAR0, 2, 2), (act, NEAR0, 10, 2), (act, OWN01, 6, 2), (mm1, OWN01, 4, 2), (w_t, 2, 6),
+        (act, NEAR0, 4, 2), (act, OWN01, 0, 2), (act, FAR0, 8, 2), (w_t, 2, 5), (rsz, 1, 0), (w_t, 2, 3), (w_t, 2, 7),
+        (act, FAR0, 6, 2), (rs1n, 1, 0), (act, FAR0, 0, 2), (mm2, REST0, 0), (w_t, 2, 4), (rs1n, 0, 0), (rs1o, 0, 0),
+        (act, OWN23, 2, 2), (rs1o, 1, 0), (w_t, 2, 8), (mm1, OWN01, 10, 2), (rsz, 0, 0), (mm1, NEAR3Z1, 0, 12),
+        (mm2, REST1, 1), (rsz, 1, 1), (rs1, 0, 0), (act, REST2, 6, 6), (rs1n, 1, 1), (mm2, REST0, 1), (rs1, 1, 0),
+        (rs1o, 0, 1), (rsz, 0, 1), (mm1, OWN23Z1, 4, 8), (mm1, NEAR3Z0, 6, 6), (rs1n, 0, 1), (rs1, 1, 1), (rs2, 0, 0),
+        (act, REST2, 0, 6), (mm2, REST2, 0), (rs1n, 2, 0), (mm2, REST2, 1), (rs1o, 1, 1), (mm1, NEAR3Z0, 0, 6),
+        (rs1o, 2, 1), (rs1, 0, 1), (rsz, 2, 1), (act, FAR3, 0, 12), (mm2, FAR3, 0), (rsz, 2, 0), (rs2, 1, 1),
+        (mm2, FAR3, 1), (rsz, 3, 1), (rsz, 3, 0), (rs2, 1, 0), (rs1n, 2, 1), (mm1, OWN23Z0, 8, 4), (mm1, OWN23Z0, 4, 4),
+        (rs1, 2, 1), (act, OWN01, 4, 2), (act, OWN01, 8, 2), (act, OWN01, 10, 2), (rs1o, 2, 0), (mm2, OWN01, 1),
+        (rs1, 2, 0), (rs3, 1, 1), (mm2, OWN01, 0), (rs3, 0, 0), (rs2, 0, 1), (act, NEAR3Z1, 0, 12), (rs3, 1, 0),
+        (rs1, 3, 1), (mm2, NEAR3Z1, 1), (rs2, 2, 1), (rs1, 3, 0), (mm2, NEAR3Z1, 0), (rs1n, 3, 0), (act, OWN23Z1, 4, 8),
+        (rs1n, 3, 1), (rs4, 1, 1), (rs3, 0, 1), (mm2, OWN23Z1, 1), (rs2, 2, 0), (rs3, 2, 1), (rs4, 0, 0), (mm2, OWN23Z1, 0),
+        (rs4, 1, 0), (rs3, 2, 0), (act, NEAR3Z0, 6, 6), (act, NEAR3Z0, 0, 6), (mm2, NEAR3Z0, 0), (rs1o, 3, 0), (rs3, 3, 0),
+        (rs2, 3, 0), (rs4, 0, 1), (mm2, NEAR3Z0, 1), (rs1o, 3, 1), (act, OWN23Z0, 8, 4), (rs2, 3, 1), (rs3, 3, 1),
+        (act, OWN23Z0, 4, 4), (mm2, OWN23Z0, 0), (rs4, 2, 0), (mm2, OWN23Z0, 1), (rs4, 2, 1), (rs4, 3, 0), (rs4, 3, 1),
     ]
     for copy in [load_tok] + vectors:
         copy.wait()

time: 101 us -> 102 us (level)
  Pallas kernels: 99.9 us -> 101 us
where the time goes in v2:
time: 102 us
  Pallas kernels  101 us (99%)
    pallas_call x1, Pallas kernels, local(): pl.pallas_call(functools.partial(kernel, (tq, kb, nf)), out_shape=jax.Sha...  101 us

profile of v2, /device:TPU:0, one launch (start us, length us, event | category | flops | bytes accessed | tf_op | source)
XLA Modules:
  0.0 101.5 jit_solution(11981334989078749646)
XLA Ops:
  0.0 0.0 copy-start
  0.0 100.6 %shard_map.64 = bf16[64,4608]{1,0:T(8,128)(2,1)S(1)} custom-call(bf16[64,4608]{1,0:T(8,128)(2,1)} %tok_hbm.1, f32[4608]{0:T(1024)} %gain_hbm.1, bf16[1152,1536]{1,0:T(8,128)(2,1)} %w1_hbm.1, f32[1536]{0:T(1024)} %b1_hbm.1, bf16[1536,1152]{1,0:T(8,128)(2,1)} %w2_hbm.1, f32[1152]{0:T(1024)} %b2_hbm.1), custom_call_target="tpu_custom_call" | custom-call | flops 14495514624 | bytes 7077888 | tf_op jit(solution)/shard_map/pallas_call | solution.py:375
  100.6 0.0 copy-done
  100.6 1.0 add_convert_fusion
Async XLA Ops:
  0.0 100.6 %copy-start = (bf16[64,4608]{1,0:T(8,128)(2,1)S(1)}, bf16[64,4608]{1,0:T(8,128)(2,1)}, u32[]{:S(2)}) copy-start(bf16[64,4608]{1,0:T(8,128)(2,1)} %tok_hbm.1) | copy-start | bytes 1769476

commit v3 on v2

--- a/solution.py
+++ b/solution.py
@@ -10,11 +10,11 @@
 MESH = pl.DeviceIdType.MESH
 F32, BF16 = jnp.float32, jnp.bfloat16
 NQ = 4
-N_RECV = 158
+N_RECV = 156
 SQRT_HALF = 0.7071067811865476
 OWN, UP, DOWN, FAR = 0, 1, 2, 3
 C1 = 128
-W1_CHUNKS = ((0, 2, 4), (2, 2, 2), (4, 2, 4), (6, 2, 2), (8, 2, 4), (10, 2, 4))
+W1_CHUNKS = ((0, 2, 4), (2, 2, 2), (4, 2, 4), (6, 2, 2), (8, 2, 4), (10, 2, 2))
 NW2 = 9
 Z = (0, 2)
 OWN01, NEAR0, FAR0 = ((0, 1), (0, 2), Z), ((1, 3), (0, 1), Z), ((3, 4), (0, 1), Z)
@@ -314,34 +314,34 @@
         pltpu.make_async_copy(fr.at[h, rows], there, local_sems.at[3]).start()
 
     order = [
-        (ag_y, 0), (ag_y, 1), (ag_x00, 0), (ag_y, 3), (ag_y, 2), (ag_x00, 3), (ag_z, 0), (w_y, 1, 0), (ag_z, 1), (ag_z, 3),
-        (ag_x00, 1), (ag_z, 2), (ag_x0, 0), (ag_x1, 0), (w_y, 1, 1), (ag_x0, 1), (w_t, 1, 0), (ag_x1, 1),
-        (mm1, OWN01, 2, 2), (ag_fd, 0), (w_y, 1, 2), (mm1, OWN01, 0, 2), (mm1, NEAR0, 2, 2), (ag_fu, 0), (mm1, NEAR0, 0, 2),
-        (ag_fd, 1), (mm1, OWN23, 0, 2), (ag_fu, 1), (w_y, 1, 3), (ag_x00, 2), (mm1, OWN23, 2, 2), (mm1, FAR0, 0, 2),
-        (ag_x0, 2), (mm1, FAR0, 2, 2), (w_y, 1, 4), (w_t, 1, 2), (mm1, FAR0, 6, 2), (mm1, NEAR0, 6, 2), (ag_x1, 2),
-        (mm1, OWN01, 6, 2), (w_y, 1, 5), (mm1, REST1, 0, 4), (ag_x0, 3), (w_y, 2, 0), (w_t, 1, 4), (w_y, 2, 1),
-        (mm1, REST1, 4, 4), (w_y, 2, 2), (ag_x1, 3), (act, NEAR0, 6, 2), (w_t, 1, 5), (w_y, 2, 3), (mm1, NEAR0, 8, 2),
-        (mm1, NEAR0, 4, 2), (ag_fu, 2), (act, NEAR0, 0, 2), (ag_fu, 3), (mm1, FAR0, 4, 2), (mm1, FAR0, 8, 2),
-        (act, NEAR0, 2, 2), (ag_fd, 2), (mm1, REST1, 8, 4), (w_y, 2, 5), (ag_fd, 3), (mm1, FAR0, 10, 2), (act, OWN01, 2, 2),
-        (act, REST1, 4, 4), (w_y, 2, 6), (mm1, NEAR0, 10, 2), (w_y, 2, 4), (mm1, REST2, 6, 6), (w_y, 2, 7),
-        (act, REST1, 0, 4), (mm1, REST2, 0, 6), (act, OWN23, 0, 2), (w_y, 2, 8), (mm1, FAR3, 0, 12), (act, REST1, 8, 4),
-        (w_t, 2, 0), (mm2, REST1, 0), (w_t, 2, 2), (act, FAR0, 10, 2), (act, FAR0, 4, 2), (act, NEAR0, 8, 2), (w_t, 2, 1),
-        (mm1, OWN01, 8, 2), (act, FAR0, 2, 2), (act, NEAR0, 10, 2), (act, OWN01, 6, 2), (mm1, OWN01, 4, 2), (w_t, 2, 6),
-        (act, NEAR0, 4, 2), (act, OWN01, 0, 2), (act, FAR0, 8, 2), (w_t, 2, 5), (rsz, 1, 0), (w_t, 2, 3), (w_t, 2, 7),
-        (act, FAR0, 6, 2), (rs1n, 1, 0), (act, FAR0, 0, 2), (mm2, REST0, 0), (w_t, 2, 4), (rs1n, 0, 0), (rs1o, 0, 0),
-        (act, OWN23, 2, 2), (rs1o, 1, 0), (w_t, 2, 8), (mm1, OWN01, 10, 2), (rsz, 0, 0), (mm1, NEAR3Z1, 0, 12),
-        (mm2, REST1, 1), (rsz, 1, 1), (rs1, 0, 0), (act, REST2, 6, 6), (rs1n, 1, 1), (mm2, REST0, 1), (rs1, 1, 0),
-        (rs1o, 0, 1), (rsz, 0, 1), (mm1, OWN23Z1, 4, 8), (mm1, NEAR3Z0, 6, 6), (rs1n, 0, 1), (rs1, 1, 1), (rs2, 0, 0),
-        (act, REST2, 0, 6), (mm2, REST2, 0), (rs1n, 2, 0), (mm2, REST2, 1), (rs1o, 1, 1), (mm1, NEAR3Z0, 0, 6),
-        (rs1o, 2, 1), (rs1, 0, 1), (rsz, 2, 1), (act, FAR3, 0, 12), (mm2, FAR3, 0), (rsz, 2, 0), (rs2, 1, 1),
-        (mm2, FAR3, 1), (rsz, 3, 1), (rsz, 3, 0), (rs2, 1, 0), (rs1n, 2, 1), (mm1, OWN23Z0, 8, 4), (mm1, OWN23Z0, 4, 4),
-        (rs1, 2, 1), (act, OWN01, 4, 2), (act, OWN01, 8, 2), (act, OWN01, 10, 2), (rs1o, 2, 0), (mm2, OWN01, 1),
-        (rs1, 2, 0), (rs3, 1, 1), (mm2, OWN01, 0), (rs3, 0, 0), (rs2, 0, 1), (act, NEAR3Z1, 0, 12), (rs3, 1, 0),
-        (rs1, 3, 1), (mm2, NEAR3Z1, 1), (rs2, 2, 1), (rs1, 3, 0), (mm2, NEAR3Z1, 0), (rs1n, 3, 0), (act, OWN23Z1, 4, 8),
-        (rs1n, 3, 1), (rs4, 1, 1), (rs3, 0, 1), (mm2, OWN23Z1, 1), (rs2, 2, 0), (rs3, 2, 1), (rs4, 0, 0), (mm2, OWN23Z1, 0),
-        (rs4, 1, 0), (rs3, 2, 0), (act, NEAR3Z0, 6, 6), (act, NEAR3Z0, 0, 6), (mm2, NEAR3Z0, 0), (rs1o, 3, 0), (rs3, 3, 0),
-        (rs2, 3, 0), (rs4, 0, 1), (mm2, NEAR3Z0, 1), (rs1o, 3, 1), (act, OWN23Z0, 8, 4), (rs2, 3, 1), (rs3, 3, 1),
-        (act, OWN23Z0, 4, 4), (mm2, OWN23Z0, 0), (rs4, 2, 0), (mm2, OWN23Z0, 1), (rs4, 2, 1), (rs4, 3, 0), (rs4, 3, 1),
+        (ag_y, 0), (ag_x00, 3), (ag_x00, 0), (ag_z, 0), (ag_x0, 0), (ag_x00, 2), (ag_y, 3), (ag_x00, 1), (ag_y, 1),
+        (w_y, 1, 0), (ag_x1, 0), (ag_y, 2), (ag_x0, 1), (ag_fu, 0), (ag_z, 1), (w_t, 1, 0), (ag_z, 2), (w_y, 1, 1),
+        (ag_fd, 0), (ag_z, 3), (mm1, NEAR0, 0, 2), (mm1, NEAR0, 2, 2), (mm1, OWN01, 0, 2), (ag_x0, 2), (w_y, 1, 2),
+        (ag_x1, 1), (mm1, OWN01, 2, 2), (mm1, FAR0, 0, 2), (mm1, FAR0, 2, 2), (mm1, OWN23, 2, 2), (ag_fu, 1), (w_y, 1, 3),
+        (mm1, OWN23, 0, 2), (ag_fd, 1), (act, FAR0, 2, 2), (mm1, FAR0, 6, 2), (w_t, 1, 2), (ag_x1, 2), (mm1, NEAR0, 6, 2),
+        (ag_x1, 3), (w_y, 1, 4), (mm1, OWN01, 6, 2), (mm1, NEAR0, 4, 2), (act, FAR0, 0, 2), (mm1, REST1, 0, 4), (w_t, 1, 4),
+        (w_y, 1, 5), (mm1, REST1, 4, 4), (w_y, 2, 0), (act, OWN23, 0, 2), (ag_fu, 2), (act, NEAR0, 4, 2), (mm1, FAR0, 4, 2),
+        (ag_x0, 3), (w_y, 2, 1), (act, OWN01, 0, 2), (mm1, REST1, 8, 4), (ag_fd, 2), (w_y, 2, 2), (act, NEAR0, 0, 2),
+        (act, REST1, 0, 4), (ag_fd, 3), (mm1, FAR0, 8, 2), (mm1, NEAR0, 8, 2), (act, OWN01, 2, 2), (mm1, FAR0, 10, 2),
+        (w_y, 2, 3), (mm1, NEAR0, 10, 2), (w_y, 2, 4), (ag_fu, 3), (w_y, 2, 5), (mm1, REST2, 6, 6), (w_t, 2, 0),
+        (act, FAR0, 4, 2), (mm1, OWN01, 4, 2), (w_y, 2, 6), (mm1, REST2, 0, 6), (act, FAR0, 8, 2), (act, REST1, 8, 4),
+        (w_t, 2, 2), (act, NEAR0, 2, 2), (act, FAR0, 6, 2), (mm1, OWN01, 8, 2), (w_y, 2, 7), (act, NEAR0, 8, 2),
+        (act, REST1, 4, 4), (mm2, REST1, 0), (w_y, 2, 8), (act, NEAR0, 10, 2), (w_t, 2, 5), (act, FAR0, 10, 2),
+        (act, NEAR0, 6, 2), (mm2, REST0, 0), (w_t, 2, 3), (rsz, 0, 0), (mm1, OWN01, 10, 2), (w_t, 2, 4), (w_t, 2, 1),
+        (rs1o, 0, 0), (rsz, 1, 0), (rs1n, 0, 0), (rs1o, 1, 0), (mm1, FAR3, 0, 12), (rs1n, 1, 0), (w_t, 2, 6), (w_t, 2, 8),
+        (w_t, 2, 7), (mm1, NEAR3Z1, 0, 12), (mm2, REST0, 1), (rs1, 0, 0), (rsz, 0, 1), (rs1n, 0, 1), (mm2, REST1, 1),
+        (act, OWN01, 6, 2), (rs1, 1, 0), (act, REST2, 6, 6), (mm1, OWN23Z1, 4, 8), (rs1n, 1, 1), (rs1o, 1, 1), (rsz, 1, 1),
+        (rs1o, 0, 1), (mm1, NEAR3Z0, 6, 6), (act, REST2, 0, 6), (mm2, REST2, 1), (rsz, 2, 1), (rs2, 1, 0), (rs1, 0, 1),
+        (act, OWN23, 2, 2), (mm2, REST2, 0), (rs1, 1, 1), (rs1n, 2, 1), (rs1n, 2, 0), (act, OWN01, 8, 2),
+        (act, OWN01, 4, 2), (rs2, 0, 0), (act, OWN01, 10, 2), (mm2, OWN01, 0), (rs3, 1, 0), (mm1, NEAR3Z0, 0, 6),
+        (rsz, 2, 0), (mm1, OWN23Z0, 8, 4), (act, FAR3, 0, 12), (mm2, FAR3, 0), (rsz, 3, 0), (rs2, 0, 1), (rs1o, 2, 0),
+        (mm1, OWN23Z0, 4, 4), (rs4, 1, 0), (rs2, 1, 1), (rs3, 0, 0), (mm2, FAR3, 1), (rs1, 2, 1), (rsz, 3, 1), (rs1, 2, 0),
+        (mm2, OWN01, 1), (act, NEAR3Z1, 0, 12), (rs1, 3, 0), (rs3, 1, 1), (mm2, NEAR3Z1, 0), (rs1n, 3, 0), (rs4, 0, 0),
+        (rs3, 0, 1), (mm2, NEAR3Z1, 1), (act, OWN23Z1, 4, 8), (rs1n, 3, 1), (mm2, OWN23Z1, 1), (rs3, 2, 1),
+        (act, NEAR3Z0, 6, 6), (rs1, 3, 1), (rs2, 2, 1), (rs2, 2, 0), (rs4, 1, 1), (mm2, OWN23Z1, 0), (rs3, 2, 0),
+        (rs1o, 2, 1), (act, NEAR3Z0, 0, 6), (rs4, 0, 1), (rs3, 3, 0), (mm2, NEAR3Z0, 0), (rs2, 3, 0), (rs1o, 3, 0),
+        (mm2, NEAR3Z0, 1), (act, OWN23Z0, 8, 4), (rs2, 3, 1), (rs1o, 3, 1), (rs3, 3, 1), (act, OWN23Z0, 4, 4),
+        (mm2, OWN23Z0, 0), (rs4, 2, 0), (mm2, OWN23Z0, 1), (rs4, 2, 1), (rs4, 3, 0), (rs4, 3, 1),
     ]
     for copy in [load_tok] + vectors:
         copy.wait()

time: 102 us -> 101 us (level)
  Pallas kernels: 101 us -> 99.6 us
where the time goes in v3:
time: 101 us
  Pallas kernels  99.6 us (99%)
    pallas_call x1, Pallas kernels, local(): pl.pallas_call(functools.partial(kernel, (tq, kb, nf)), out_shape=jax.Sha...  99.6 us

profile of v3, /device:TPU:0, one launch (start us, length us, event | category | flops | bytes accessed | tf_op | source)
XLA Modules:
  0.0 100.6 jit_solution(3252537569449233291)
XLA Ops:
  0.0 0.0 copy-start
  0.0 99.6 %shard_map.64 = bf16[64,4608]{1,0:T(8,128)(2,1)S(1)} custom-call(bf16[64,4608]{1,0:T(8,128)(2,1)} %tok_hbm.1, f32[4608]{0:T(1024)} %gain_hbm.1, bf16[1152,1536]{1,0:T(8,128)(2,1)} %w1_hbm.1, f32[1536]{0:T(1024)} %b1_hbm.1, bf16[1536,1152]{1,0:T(8,128)(2,1)} %w2_hbm.1, f32[1152]{0:T(1024)} %b2_hbm.1), custom_call_target="tpu_custom_call" | custom-call | flops 14495514624 | bytes 7077888 | tf_op jit(solution)/shard_map/pallas_call | solution.py:375
  99.6 0.0 copy-done
  99.6 1.0 add_convert_fusion
Async XLA Ops:
  0.0 99.6 %copy-start = (bf16[64,4608]{1,0:T(8,128)(2,1)S(1)}, bf16[64,4608]{1,0:T(8,128)(2,1)}, u32[]{:S(2)}) copy-start(bf16[64,4608]{1,0:T(8,128)(2,1)} %tok_hbm.1) | copy-start | bytes 1769476
